TPU v7x, 128 devices: a whole 4x4x4 slice. The times are simulated.
128 devices in a mesh: ens: 1, part: 16 (over z, y), feat: 8 (over x, core).
Axes of the slice: x: 4, y: 4, z: 4, core: 2. Of those that a mesh axis runs over, the one named last changes fastest.
Arguments:
- particles: float32 [2048, 32768], P(('ens', 'part'), 'feat')
- prec_diag: float32 [32768], P(('ens', 'feat'))
- target_mean: float32 [32768], P(('ens', 'feat'))
- low_factor: bfloat16 [32768, 64], P(('ens', 'feat'))
Outputs:
- output: float32 [2048, 32768], P(('ens', 'part'), 'feat')
All inputs are finite; a program needn't handle non-finite values.
Results may differ from a plain program's by a relative error of at most 0.00350775.
Values are sent between devices in bfloat16 or wider.
A program may use at most 1 GiB of HBM per device.

v0:
```python
import math
import jax
import jax.numpy as jnp
from jax import lax
from jax.sharding import PartitionSpec as P

NUM_STEPS = 3


def solution(mesh):
    part_size = mesh.shape["part"]
    feat_size = mesh.shape["feat"]

    def local_steps(local_theta, prec_loc, mean_loc, factor_loc):
        rows_loc, feat_loc = local_theta.shape
        n_total = rows_loc * part_size
        feat_total = feat_loc * feat_size
        kern_width = 2.0 * feat_total / math.log(n_total)
        step_size = 0.15 * n_total * feat_total / math.log(n_total)
        row_start = lax.axis_index("part") * rows_loc
        cur_theta = local_theta
        for step_idx in range(NUM_STEPS):
            x_dev = cur_theta - mean_loc[None, :]
            proj_part = jnp.dot(x_dev.astype(jnp.bfloat16), factor_loc, preferred_element_type=jnp.float32)
            proj_low = lax.psum(proj_part, "feat")
            low_term = jnp.einsum("nr,dr->nd", proj_low.astype(jnp.bfloat16), factor_loc, preferred_element_type=jnp.float32)
            grad_b = (-(x_dev * prec_loc[None, :] + low_term)).astype(jnp.bfloat16)
            theta_b = cur_theta.astype(jnp.bfloat16)
            theta_all = lax.all_gather(theta_b, "part", axis=0, tiled=True)
            gram_part = jnp.einsum("nd,md->nm", theta_b, theta_all, preferred_element_type=jnp.float32)
            sq_part = jnp.einsum("md,md->m", theta_all, theta_all, preferred_element_type=jnp.float32)
            gram_rows, sq_norm = lax.psum((gram_part, sq_part), "feat")
            sq_own = lax.dynamic_slice_in_dim(sq_norm, row_start, rows_loc)
            sq_dist = jnp.maximum(sq_own[:, None] + sq_norm[None, :] - 2.0 * gram_rows, 0.0)
            kern_b = jnp.exp(-sq_dist / kern_width).astype(jnp.bfloat16)
            row_mass = jnp.sum(kern_b, axis=1, dtype=jnp.float32)
            grad_all = lax.all_gather(grad_b, "part", axis=0, tiled=True)
            drive_term = jnp.dot(kern_b, grad_all, preferred_element_type=jnp.float32)
            pull_term = jnp.dot(kern_b, theta_all, preferred_element_type=jnp.float32)
            update_dir = (drive_term + (2.0 / kern_width) * (row_mass[:, None] * theta_b.astype(jnp.float32) - pull_term)) / n_total
            cur_theta = cur_theta + step_size * update_dir
        return cur_theta

    row_spec = P(("ens", "part"), "feat")
    vec_spec = P(("ens", "feat"))
    fac_spec = P(("ens", "feat"), None)
    return jax.shard_map(local_steps, mesh=mesh, in_specs=(row_spec, vec_spec, vec_spec, fac_spec), out_specs=row_spec, check_vma=False)
```

profile of v0, /device:TPU:0, one launch (start us, length us, event | category | flops | bytes accessed | tf_op | source)
XLA Modules:
  0.0 967.6 jit_solution(7713996670019497685)
XLA Ops:
  6.5 2.8 convert_element_type.63
  9.9 113.1 %all-gather.7.cloned.1.call-done = bf16[2048,4096]{1,0:T(8,128)(2,1)} async-done(((bf16[128,4096]{1,0:T(8,128)(2,1)}), bf16[2048,4096]{1,0:T(8,128)(2,1)}) %all-gather.7.cloned.1.call-update) | async-done | bytes 16777232 | tf_op jit(solution)/shard_map/all_gather | solution.py:29
  123.1 12.4 %fusion.32 = f32[128,2048]{1,0:T(8,128)} fusion(bf16[2048,4096]{1,0:T(8,128)(2,1)} %all-gather.7.cloned.1.call-done, f32[128,4096]{1,0:T(8,128)S(1)} %copy-done.1), kind=kOutput, calls=%fused_computation.50 | convolution fusion | flops 2148007936 | bytes 19922944 | tf_op jit(solution)/shard_map/nd,md->nm/dot_general | solution.py:30
  135.5 7.2 fusion.2
  142.7 26.2 %all-reduce.2 = (f32[2048]{0:T(1024)S(1)}, bf16[128,64]{1,0:T(8,128)(2,1)S(1)}) all-reduce(f32[2048]{0:T(1024)S(1)} %fusion.2, f32[128,64]{1,0:T(8,128)S(1)} %fusion.21), channel_id=1, replica_groups=mesh['ens'=1,'part'=16,'feat'=8] {'feat'}, use_global_device_ids=true, to_apply=%region_0.0 | all-reduce | flops 10240 | bytes 65536 | tf_op jit(solution)/shard_map/psum | solution.py:32
  168.9 1.5 fusion.18
  170.6 27.3 %all-reduce.7.cloned.1.call-done = f32[128,2048]{1,0:T(8,128)} async-done(((f32[128,2048]{1,0:T(8,128)}), f32[128,2048]{1,0:T(8,128)}) %all-reduce.7.cloned.1.call-update) | async-done | bytes 1048592 | tf_op jit(solution)/shard_map/psum | solution.py:32
  197.8 1.7 convert_reduce_fusion.2
  199.5 110.7 %all-gather.9.cloned.1.call-done = bf16[2048,4096]{1,0:T(8,128)(2,1)} async-done(((bf16[128,4096]{1,0:T(8,128)(2,1)}), bf16[2048,4096]{1,0:T(8,128)(2,1)}) %all-gather.9.cloned.1.call-update) | async-done | bytes 16777232 | tf_op jit(solution)/shard_map/all_gather | solution.py:37
  310.2 8.1 fusion.34
  318.3 10.4 %fusion.30 = (bf16[128,4096]{1,0:T(8,128)(2,1)}, f32[128,4096]{1,0:T(8,128)}) fusion(f32[128,4096]{1,0:T(8,128)S(1)} %copy-done.1, f32[128,4096]{1,0:T(8,128)S(1)} %fusion.34, bf16[128,2048]{1,0:T(8,128)(2,1)S(1)} %get-tuple-element.16, bf16[2048,4096]{1,0:T(8,128)(2,1)} %all-gather.7.cloned.1.call-done, f32[128]{0:T(128)S(1)} %get-tuple-element.15), kind=kOutput, calls=%fused_computation.48 | convolution fusion | flops 2152202240 | bytes 24642048 | tf_op jit(solution)/shard_map/dot_general | solution.py:39
  328.9 2.1 fusion.22
  331.0 108.4 %all-gather.11.cloned.1.call-done = bf16[2048,4096]{1,0:T(8,128)(2,1)} async-done(((bf16[128,4096]{1,0:T(8,128)(2,1)}), bf16[2048,4096]{1,0:T(8,128)(2,1)}) %all-gather.11.cloned.1.call-update) | async-done | bytes 16777232 | tf_op jit(solution)/shard_map/all_gather | solution.py:29
  439.4 12.4 %fusion.35 = f32[128,2048]{1,0:T(8,128)} fusion(bf16[128,4096]{1,0:T(8,128)(2,1)S(1)} %copy-done.4, bf16[2048,4096]{1,0:T(8,128)(2,1)} %all-gather.11.cloned.1.call-done), kind=kOutput, calls=%fused_computation.53 | convolution fusion | flops 2147483648 | bytes 18874368 | tf_op jit(solution)/shard_map/nd,md->nm/dot_general | solution.py:30
  451.9 7.4 fusion.1
  459.2 26.2 %all-reduce.1 = (f32[2048]{0:T(1024)S(1)}, bf16[128,64]{1,0:T(8,128)(2,1)S(1)}) all-reduce(f32[2048]{0:T(1024)S(1)} %fusion.1, f32[128,64]{1,0:T(8,128)S(1)} %fusion.22), channel_id=1, replica_groups=mesh['ens'=1,'part'=16,'feat'=8] {'feat'}, use_global_device_ids=true, to_apply=%region_4.0 | all-reduce | flops 10240 | bytes 65536 | tf_op jit(solution)/shard_map/psum | solution.py:32
  485.4 1.4 fusion.19
  487.0 27.1 %all-reduce.9.cloned.1.call-done = f32[128,2048]{1,0:T(8,128)} async-done(((f32[128,2048]{1,0:T(8,128)}), f32[128,2048]{1,0:T(8,128)}) %all-reduce.9.cloned.1.call-update) | async-done | bytes 1048592 | tf_op jit(solution)/shard_map/psum | solution.py:32
  514.1 1.7 convert_reduce_fusion.1
  515.8 110.6 %all-gather.13.cloned.1.call-done = bf16[2048,4096]{1,0:T(8,128)(2,1)} async-done(((bf16[128,4096]{1,0:T(8,128)(2,1)}), bf16[2048,4096]{1,0:T(8,128)(2,1)}) %all-gather.13.cloned.1.call-update) | async-done | bytes 16777232 | tf_op jit(solution)/shard_map/all_gather | solution.py:37
  626.4 8.2 fusion.36
  634.6 10.4 %fusion.31 = (bf16[128,4096]{1,0:T(8,128)(2,1)}, f32[128,4096]{1,0:T(8,128)}) fusion(f32[128,4096]{1,0:T(8,128)S(1)} %copy-done.2, f32[128,4096]{1,0:T(8,128)S(1)} %fusion.36, bf16[128,2048]{1,0:T(8,128)(2,1)S(1)} %get-tuple-element.14, bf16[2048,4096]{1,0:T(8,128)(2,1)} %all-gather.11.cloned.1.call-done, bf16[128,4096]{1,0:T(8,128)(2,1)S(1)} %copy-done.5, ...), kind=kOutput, calls=%fused_computation.49 | convolution fusion | flops 2151677952 | bytes 25690624 | tf_op jit(solution)/shard_map/dot_general | solution.py:39
  645.3 2.0 fusion.23
  647.3 108.4 %all-gather.15.cloned.1.call-done = bf16[2048,4096]{1,0:T(8,128)(2,1)} async-done(((bf16[128,4096]{1,0:T(8,128)(2,1)}), bf16[2048,4096]{1,0:T(8,128)(2,1)}) %all-gather.15.cloned.1.call-update) | async-done | bytes 16777232 | tf_op jit(solution)/shard_map/all_gather | solution.py:29
  755.7 12.4 %fusion.37 = f32[128,2048]{1,0:T(8,128)} fusion(bf16[128,4096]{1,0:T(8,128)(2,1)S(1)} %copy-done.6, bf16[2048,4096]{1,0:T(8,128)(2,1)} %all-gather.15.cloned.1.call-done), kind=kOutput, calls=%fused_computation.55 | convolution fusion | flops 2147483648 | bytes 18874368 | tf_op jit(solution)/shard_map/nd,md->nm/dot_general | solution.py:30
  768.1 7.4 fusion
  775.5 26.2 %all-reduce = (f32[2048]{0:T(1024)S(1)}, bf16[128,64]{1,0:T(8,128)(2,1)S(1)}) all-reduce(f32[2048]{0:T(1024)S(1)} %fusion, f32[128,64]{1,0:T(8,128)S(1)} %fusion.23), channel_id=1, replica_groups=mesh['ens'=1,'part'=16,'feat'=8] {'feat'}, use_global_device_ids=true, to_apply=%region_8.0 | all-reduce | flops 10240 | bytes 65536 | tf_op jit(solution)/shard_map/psum | solution.py:32
  803.2 27.2 %all-reduce.11.cloned.1.call-done = f32[128,2048]{1,0:T(8,128)} async-done(((f32[128,2048]{1,0:T(8,128)}), f32[128,2048]{1,0:T(8,128)}) %all-reduce.11.cloned.1.call-update) | async-done | bytes 1048592 | tf_op jit(solution)/shard_map/psum | solution.py:32
  830.4 1.7 convert_reduce_fusion
  832.1 110.7 %all-gather.17.cloned.1.call-done = bf16[2048,4096]{1,0:T(8,128)(2,1)} async-done(((bf16[128,4096]{1,0:T(8,128)(2,1)}), bf16[2048,4096]{1,0:T(8,128)(2,1)}) %all-gather.17.cloned.1.call-update) | async-done | bytes 16777232 | tf_op jit(solution)/shard_map/all_gather | solution.py:37
  942.8 8.2 fusion.38
  951.0 10.0 %fusion.9 = f32[128,4096]{1,0:T(8,128)} fusion(f32[128,4096]{1,0:T(8,128)S(1)} %copy-done.3, f32[128,4096]{1,0:T(8,128)S(1)} %fusion.38, bf16[128,2048]{1,0:T(8,128)(2,1)S(1)} %get-tuple-element.12, bf16[2048,4096]{1,0:T(8,128)(2,1)} %all-gather.15.cloned.1.call-done, bf16[128,4096]{1,0:T(8,128)(2,1)S(1)} %copy-done.7, f32[128]{0:T(128)S(1)} %get-tuple-element.11), kind=kOutput, calls=%fused_computation.16 | convolution fusion | flops 2151153664 | bytes 24642048 | tf_op jit(solution)/shard_map/dot_general | solution.py:39
  (43 shorter events, 3.0 us)
Async XLA Ops:
  6.5 2.9 copy-start
  6.5 2.9 copy-start.1
  6.5 2.9 copy-start.8
  6.5 116.5 %all-gather.7.cloned.1.call-start = ((), (), s32[]{:S(2)}) async-start(), calls=%async_computation | async-start | bytes 17825792 | tf_op jit(solution)/shard_map/all_gather | solution.py:29
  9.4 188.4 %all-reduce.7.cloned.1.call-start = ((), (), s32[]{:S(2)}) async-start(), calls=%async_computation.1 | async-start | bytes 2097152 | tf_op jit(solution)/shard_map/psum | solution.py:32
  135.4 33.5 %copy-start.9 = (f32[4096]{0:T(1024)S(1)}, f32[4096]{0:T(1024)}, u32[]{:S(2)}) copy-start(f32[4096]{0:T(1024)} %param.5) | copy-start | bytes 49156
  135.4 174.7 %all-gather.9.cloned.1.call-start = ((), (), s32[]{:S(2)}) async-start(), calls=%async_computation.2 | async-start | bytes 17825792 | tf_op jit(solution)/shard_map/all_gather | solution.py:37
  170.4 269.0 %all-gather.11.cloned.1.call-start = ((), (), s32[]{:S(2)}) async-start(), calls=%async_computation.3 | async-start | bytes 17825792 | tf_op jit(solution)/shard_map/all_gather | solution.py:29
  328.7 110.7 %copy-start.4 = (bf16[128,4096]{1,0:T(8,128)(2,1)S(1)}, bf16[128,4096]{1,0:T(8,128)(2,1)}, u32[]{:S(2)}) copy-start(bf16[128,4096]{1,0:T(8,128)(2,1)} %get-tuple-element.17) | copy-start | bytes 3145732
  328.7 185.4 %all-reduce.9.cloned.1.call-start = ((), (), s32[]{:S(2)}) async-start(), calls=%async_computation.4 | async-start | bytes 2097152 | tf_op jit(solution)/shard_map/psum | solution.py:32
  451.8 33.6 %copy-start.2 = (f32[128,4096]{1,0:T(8,128)S(1)}, f32[128,4096]{1,0:T(8,128)}, u32[]{:S(2)}) copy-start(f32[128,4096]{1,0:T(8,128)} %get-tuple-element.18) | copy-start | bytes 6291460
  451.8 174.6 %all-gather.13.cloned.1.call-start = ((), (), s32[]{:S(2)}) async-start(), calls=%async_computation.5 | async-start | bytes 17825792 | tf_op jit(solution)/shard_map/all_gather | solution.py:37
  486.9 268.8 %all-gather.15.cloned.1.call-start = ((), (), s32[]{:S(2)}) async-start(), calls=%async_computation.6 | async-start | bytes 17825792 | tf_op jit(solution)/shard_map/all_gather | solution.py:29
  626.4 8.2 copy-start.5
  645.0 110.7 %copy-start.6 = (bf16[128,4096]{1,0:T(8,128)(2,1)S(1)}, bf16[128,4096]{1,0:T(8,128)(2,1)}, u32[]{:S(2)}) copy-start(bf16[128,4096]{1,0:T(8,128)(2,1)} %get-tuple-element.19) | copy-start | bytes 3145732
  645.0 185.4 %all-reduce.11.cloned.1.call-start = ((), (), s32[]{:S(2)}) async-start(), calls=%async_computation.7 | async-start | bytes 2097152 | tf_op jit(solution)/shard_map/psum | solution.py:32
  768.1 33.6 %copy-start.3 = (f32[128,4096]{1,0:T(8,128)S(1)}, f32[128,4096]{1,0:T(8,128)}, u32[]{:S(2)}) copy-start(f32[128,4096]{1,0:T(8,128)} %get-tuple-element.20) | copy-start | bytes 6291460
  768.1 174.7 %all-gather.17.cloned.1.call-start = ((), (), s32[]{:S(2)}) async-start(), calls=%async_computation.8 | async-start | bytes 17825792 | tf_op jit(solution)/shard_map/all_gather | solution.py:37
  942.8 8.2 copy-start.7
Sparse Core Ops, SparseCore 0:
  9.5 113.4 all-gather.6
  135.6 62.2 all-reduce.6
  200.0 110.1 all-gather.8
  328.8 110.5 all-gather.10
  451.9 62.1 all-reduce.8
  516.1 110.1 all-gather.12
  645.1 110.5 all-gather.14
  768.2 62.1 all-reduce.10
  832.6 110.1 all-gather.16
where the time goes:
time: 969 us; the launch traced here: 968 us
  waiting for transfers between devices  744 us (77%)
  matrix products  101 us (10%)
  blocking collectives  78.6 us (8%)
  other arithmetic  29.7 us (3%)
  between operations  13.4 us (1%)
    all_gather x3, waiting for transfers between devices, local_steps(): grad_all = lax.all_gather(grad_b, 'part', axis=0, tiled=True)  332 us
    all_gather x3, waiting for transfers between devices, local_steps(): theta_all = lax.all_gather(theta_b, 'part', axis=0, tiled=True)  330 us
    psum x3, waiting for transfers between devices, local_steps(): gram_rows, sq_norm = lax.psum((gram_part, sq_part), 'feat')  81.6 us
    psum x3, blocking collectives, local_steps(): gram_rows, sq_norm = lax.psum((gram_part, sq_part), 'feat')  78.6 us
    dot_general x3, matrix products, local_steps(): jnp.einsum('nd,md->nm', theta_b, theta_all, preferred_element_type=jnp.fl...  37.1 us
    dot_general x3, matrix products, local_steps(): pull_term = jnp.dot(kern_b, theta_all, preferred_element_type=jnp.float32)  30.8 us
    dot_general x3, matrix products, local_steps(): drive_term = jnp.dot(kern_b, grad_all, preferred_element_type=jnp.float32)  24.5 us
    dot_general x3, other arithmetic, local_steps(): jnp.einsum('md,md->m', theta_all, theta_all, preferred_element_type=jnp.f...  21.9 us
  transfers between devices with their start and end apart: 9, of which 9 were waited for; matrix products, arithmetic and copies ran while one was open for 4% of the time, Pallas kernels for 0%

commit v1 on v0

v1 whole, which is shorter than its diff:
```python
import functools
import math
import jax
import jax.numpy as jnp
from jax import lax
from jax.experimental import pallas as pl
from jax.experimental.pallas import tpu as pltpu
from jax.sharding import PartitionSpec as P

NUM_STEPS = 3
B = 128
PIECE = 48
F32 = jnp.float32
BF16 = jnp.bfloat16
NT = (((1,), (1,)), ((), ()))
TN = (((0,), (0,)), ((), ()))
NUM_SEMS = 160


def rem(a, n):
    return lax.rem(a, n)


def steps_kernel(cfg, theta_ref, lam_ref, mu_ref, fac_ref, fact_ref, out_ref, t_own, t_par, a_buf, zt, zt_par, zt_b,
                 s_all, g, ring1, ring2, dir3, acc2, acc3, unit, ag, ag_par, kfull, send_sems, recv_sems):
    sizes, nb, kern_width, step_size = cfg["sizes"], cfg["nb"], cfg["kern_width"], cfg["step_size"]
    nx, ny, nz = sizes
    n_total = nb * B
    n_chip = nx * ny * nz
    part, feat = lax.axis_index("part"), lax.axis_index("feat")
    core = rem(feat, 2)
    me = (feat // 2, rem(part, ny), part // ny)

    def dev(coord, c):
        return {"part": coord[2] * ny + coord[1], "feat": coord[0] * 2 + c}

    def shifted(dim, by):
        c = list(me)
        c[dim] = rem(me[dim] + by, sizes[dim])
        return dev(c, core)

    partner = dev(me, 1 - core)
    perms = [(k, (k + 1) % 3, (k + 2) % 3) for k in range(3)]

    ids = {}

    def copy(key, src, dst, to):
        idx = ids.setdefault(key, len(ids))
        assert idx < NUM_SEMS
        return pltpu.make_async_remote_copy(
            src_ref=src, dst_ref=dst, send_sem=send_sems.at[idx], recv_sem=recv_sems.at[idx],
            device_id=to, device_id_type=pl.DeviceIdType.MESH)

    barrier = pltpu.get_barrier_semaphore()
    peers = [partner] + [shifted(d, by) for d in range(3) if sizes[d] > 1 for by in range(1, sizes[d])]
    for peer in peers:
        pl.semaphore_signal(barrier, inc=1, device_id=peer, device_id_type=pl.DeviceIdType.MESH)
    pl.semaphore_wait(barrier, len(peers))

    row = lax.broadcasted_iota(jnp.int32, (B, B), 0)
    col = lax.broadcasted_iota(jnp.int32, (B, B), 1)
    low, eye = row >= col, row == col

    def blk(i):
        return pl.ds(pl.multiple_of(i * B, B), B)

    def unit_of(c, q):
        u = c * n_chip + q
        i = rem(u, nb)
        return u, i, rem(i + u // nb + 1, nb), u >= 2 * n_chip - nb // 2

    def chip_index(k, coord):
        p = perms[k]
        return (coord[p[0]] * sizes[p[1]] + coord[p[1]]) * sizes[p[2]] + coord[p[2]]

    def coords_of(q):
        return (q // (ny * nz), rem(q // nz, ny), rem(q, nz))

    def split(n, wide):
        if n > 1:
            return (0, n // 2, 0, PIECE), (n // 2, n // 2, 0, PIECE)
        r = 32 if wide else 24
        return (0, 1, 0, r), (0, 1, r, PIECE - r)

    def part_of(ref, lead, base, half):
        return ref.at[lead, pl.ds(base + half[0], half[1]), pl.ds(half[2], half[3])]

    out_ref[...] = theta_ref[...]

    def one_step(step, carry):
        def prep(r, cc):
            rows = pl.ds(pl.multiple_of(r * 256, 256), 256)
            th = out_ref[rows]
            t_own[rows] = th.astype(BF16)
            xb = (th - mu_ref[...]).astype(BF16)
            zt[:, rows] = lax.dot_general(fact_ref[...], xb, NT, preferred_element_type=F32)
            return cc
        lax.fori_loop(0, n_total // 256, prep, 0)
        zh = zt.shape[0] // 2
        ct = copy("t", t_own, t_par, partner)
        cz = copy("z", zt.at[pl.ds(pl.multiple_of((1 - core) * zh, 8), zh)], zt_par, partner)
        ct.start()
        cz.start()
        ct.wait()
        cz.wait()

        def gram(i, j):
            return (lax.dot_general(t_own[blk(i)], t_own[blk(j)], NT, preferred_element_type=F32)
                    + lax.dot_general(t_par[blk(i)], t_par[blk(j)], NT, preferred_element_type=F32))

        def norms(i, cc):
            s = jnp.sum(jnp.where(eye, gram(i, i), 0.0), axis=0, keepdims=True)
            s_all[i] = jnp.broadcast_to(s, (8, B))
            return cc
        lax.fori_loop(0, nb, norms, 0)

        row8 = lax.broadcasted_iota(jnp.int32, (8, B), 0)

        def form(q, cc):
            u, i, j, packed = unit_of(core, q)
            coord = coords_of(q)
            i0, i1, i2 = (chip_index(k, coord) for k in range(3))
            srows = jnp.where(row8 == 0, s_all[i], s_all[j])
            zrow = u // nb
            zb = (zt[pl.ds(pl.multiple_of(zrow * 8, 8), 8), blk(i)]
                  + zt_par[pl.ds(pl.multiple_of(zrow * 8 - core * zh, 8), 8), blk(i)])
            tail = jnp.concatenate([srows, zb], 0)

            def put(m):
                g[0, i0] = m[:48]
                g[1, i1] = m[48:96]
                g[2, i2] = jnp.concatenate([m[96:], tail], 0)

            @pl.when(jnp.logical_not(packed))
            def _():
                put(gram(i, j))

            @pl.when(packed)
            def _():
                put(jnp.where(low, gram(i, i), gram(j, j)))
            return cc
        lax.fori_loop(0, n_chip, form, 0)

        pending = []
        for ph in (0, 1):
            src = (g, acc2)[ph]
            bufs = (ring1, ring2)[ph]
            dstacc = (acc2, acc3)[ph]
            active = []
            for k in range(3):
                p = perms[k]
                d = p[ph]
                n = sizes[p[2]] * (sizes[p[1]] if ph == 0 else 1)
                if sizes[d] == 1:
                    dstacc[k, pl.ds(0, n)] = src[k, pl.ds(0, n)]
                    continue
                base = [rem(me[d] + s, 4) * n for s in range(4)]
                ha, hb = split(n, False)
                key = ("rs", ph, k)
                right, left = shifted(d, 1), shifted(d, 3)
                m1p = copy(key + (0,), part_of(src, k, base[2], ha), bufs.at[k, 0, pl.ds(0, ha[1]), pl.ds(0, ha[3])], right)
                m1m = copy(key + (1,), part_of(src, k, base[2], hb), bufs.at[k, 1, pl.ds(0, hb[1]), pl.ds(0, hb[3])], left)
                m2p = copy(key + (2,), part_of(src, k, base[1], hb), part_of(bufs.at[k], 2, 0, hb), right)
                m2m = copy(key + (3,), part_of(src, k, base[3], ha), part_of(bufs.at[k], 3, 0, ha), left)
                m3p = copy(key + (4,), part_of(src, k, base[1], ha), part_of(bufs.at[k], 2, 0, ha), right)
                m3m = copy(key + (5,), part_of(src, k, base[3], hb), part_of(bufs.at[k], 3, 0, hb), left)
                for m in (m1p, m1m, m2p, m2m):
                    m.start()
                active.append((k, n, base, ha, hb, m1p, m1m, m2p, m2m, m3p, m3m))
            for k, n, base, ha, hb, m1p, m1m, m2p, m2m, m3p, m3m in active:
                m1p.wait_recv()
                part_of(src, k, base[1], ha)[...] += bufs[k, 0, pl.ds(0, ha[1]), pl.ds(0, ha[3])]
                m3p.start()
                m1m.wait_recv()
                part_of(src, k, base[3], hb)[...] += bufs[k, 1, pl.ds(0, hb[1]), pl.ds(0, hb[3])]
                m3m.start()
            for k, n, base, ha, hb, m1p, m1m, m2p, m2m, m3p, m3m in active:
                for m in (m2p, m2m, m3p, m3m):
                    m.wait_recv()

                def add(v, cc):
                    dstacc[k, v] = src[k, base[0] + v] + bufs[k, 2, v] + bufs[k, 3, v]
                    return cc
                lax.fori_loop(0, n, add, 0)
                pending += [m1p, m1m, m2p, m2m, m3p, m3m]
        active = []
        for k in range(3):
            d = perms[k][2]
            if sizes[d] == 1:
                active.append((k, d, []))
                continue
            ms = []
            for by in range(1, 4):
                m = copy(("rs", 2, k, by), acc3.at[k, rem(me[d] + by, 4)], dir3.at[k, by], shifted(d, by))
                m.start()
                ms.append(m)
            active.append((k, d, ms))
            pending += ms
        for k, d, ms in active:
            tot = acc3[k, me[d] if ms else 0]
            for m in ms:
                m.wait_recv()
            for by in range(1, len(ms) + 1):
                tot = tot + dir3[k, by]
            unit[k] = tot

        packed = unit_of(core, (me[0] * ny + me[1]) * nz + me[2])[3]
        first = jnp.logical_or(jnp.logical_not(packed), low)
        second = jnp.logical_or(jnp.logical_not(packed), jnp.logical_not(low))
        g_u = jnp.concatenate([unit[0], unit[1], unit[2, pl.ds(0, 32)]], 0)
        si = jnp.broadcast_to(unit[2, pl.ds(32, 1)], (B, B))
        sj = jnp.broadcast_to(unit[2, pl.ds(33, 1)], (B, B))
        si_c = jnp.broadcast_to(jnp.sum(jnp.where(eye, si, 0.0), axis=1, keepdims=True), (B, B))
        sj_c = jnp.broadcast_to(jnp.sum(jnp.where(eye, sj, 0.0), axis=1, keepdims=True), (B, B))
        s_sum = jnp.where(first, si_c, sj_c) + jnp.where(second, sj, si)
        dist = jnp.maximum(s_sum - 2.0 * g_u, 0.0)
        k_u = jnp.exp(-dist / kern_width)
        z_u = unit[2, pl.ds(40, 8)]
        pieces = (k_u[:48], k_u[48:96], jnp.concatenate([k_u[96:], z_u, jnp.zeros_like(z_u)], 0))
        own = [chip_index(k, me) for k in range(3)]
        for k in range(3):
            ag[k, own[k]] = pieces[k].astype(BF16)

        active = []
        for k in range(3):
            d = perms[k][2]
            if sizes[d] == 1:
                continue
            for by in range(1, 4):
                m = copy(("ag", 2, k, by), ag.at[k, own[k]], ag.at[k, own[k]], shifted(d, by))
                m.start()
                active.append(m)
        for m in active:
            m.wait_recv()
        pending += active
        swaps = []

        def swap(key, ref_of):
            m = copy(("sw",) + key, ref_of(ag), ref_of(ag_par), partner)
            m.start()
            swaps.append(m)

        for ph in (1, 0):
            active = []
            for k in range(3):
                p = perms[k]
                d = p[ph]
                n = sizes[p[2]] * (sizes[p[1]] if ph == 0 else 1)
                top = me[p[0]] * sizes[p[1]] * sizes[p[2]] if ph == 1 else 0
                base = [top + rem(me[d] + s, sizes[d]) * n for s in range(sizes[d])]
                if ph == 0:
                    swap((k, 6), lambda ref: ref.at[k, pl.ds(base[0], n)])
                if sizes[d] == 1:
                    continue
                ha, hb = split(n, True)
                right, left = shifted(d, 1), shifted(d, 3)
                key = ("ag", ph, k)

                def send(tag, b, h, to):
                    return copy(key + (tag,), part_of(ag, k, b, h), part_of(ag, k, b, h), to)
                n1p, n1m = send(0, base[0], ha, right), send(1, base[0], hb, left)
                n2p, n2m = send(2, base[0], hb, right), send(3, base[0], ha, left)
                for m in (n1p, n1m, n2p, n2m):
                    m.start()
                n3p, n3m = send(4, base[3], ha, right), send(5, base[1], hb, left)
                active.append((k, n, base, ha, hb, n1p, n1m, n2p, n2m, n3p, n3m))
            for k, n, base, ha, hb, n1p, n1m, n2p, n2m, n3p, n3m in active:
                n1p.wait_recv()
                n3p.start()
                n1m.wait_recv()
                n3m.start()
                if ph == 0:
                    swap((k, 0), lambda ref: part_of(ref, k, base[3], ha))
                    swap((k, 1), lambda ref: part_of(ref, k, base[1], hb))
            for k, n, base, ha, hb, n1p, n1m, n2p, n2m, n3p, n3m in active:
                got = ((n2p, base[3], hb), (n2m, base[1], ha), (n3p, base[2], ha), (n3m, base[2], hb))
                for t, (m, b, h) in enumerate(got):
                    m.wait_recv()
                    if ph == 0:
                        swap((k, 2 + t), lambda ref: part_of(ref, k, b, h))
                pending += [n1p, n1m, n2p, n2m, n3p, n3m]

        def assemble(ref, c):
            def body(q, cc):
                u, i, j, packed = unit_of(c, q)
                coord = coords_of(q)
                i0, i1, i2 = (chip_index(k, coord) for k in range(3))
                tail = ref[2, i2].astype(F32)
                m = jnp.concatenate([ref[0, i0].astype(F32), ref[1, i1].astype(F32), tail[:32]], 0)
                zt_b[pl.ds(pl.multiple_of(u // nb * 8, 8), 8), blk(i)] = tail[32:40]
                mt = m.T

                @pl.when(jnp.logical_not(packed))
                def _():
                    kfull[blk(i), blk(j)] = m.astype(BF16)
                    kfull[blk(j), blk(i)] = mt.astype(BF16)

                @pl.when(packed)
                def _():
                    kfull[blk(i), blk(i)] = jnp.where(eye, 1.0, jnp.where(low, m, mt)).astype(BF16)
                    kfull[blk(j), blk(j)] = jnp.where(eye, 1.0, jnp.where(low, mt, m)).astype(BF16)
                    zero = jnp.zeros((B, B), BF16)
                return cc
            lax.fori_loop(0, n_chip, body, 0)
        assemble(ag, core)
        for m in swaps:
            m.wait_recv()
        assemble(ag_par, 1 - core)

        def grads(r, cc):
            rows = pl.ds(pl.multiple_of(r * 256, 256), 256)
            lowt = lax.dot_general(zt_b[:, rows].astype(BF16), fact_ref[...], TN, preferred_element_type=F32)
            a_buf[rows] = (-((out_ref[rows] - mu_ref[...]) * lam_ref[...] + lowt)).astype(BF16)
            return cc
        lax.fori_loop(0, n_total // 256, grads, 0)

        def update(r, cc):
            rows = pl.ds(pl.multiple_of(r * 256, 256), 256)
            kr = kfull[rows]
            mass = jnp.sum(kr.astype(F32), axis=1, keepdims=True)
            drive = jnp.dot(kr, a_buf[...], preferred_element_type=F32)
            pull = jnp.dot(kr, t_own[...], preferred_element_type=F32)
            upd = (drive + (2.0 / kern_width) * (mass * t_own[rows].astype(F32) - pull)) / n_total
            out_ref[rows] = out_ref[rows] + step_size * upd
            return cc
        lax.fori_loop(0, n_total // 256, update, 0)
        for m in pending + swaps:
            m.wait_send()
        return carry

    lax.fori_loop(0, NUM_STEPS, one_step, 0)


def run_steps(theta, lam, mu, fac, sizes, kern_width, step_size):
    n_total, fcol = theta.shape
    rank = fac.shape[1]
    nb = n_total // B
    n_chip = sizes[0] * sizes[1] * sizes[2]
    assert nb * nb == 4 * n_chip and rank == 4 * nb
    cfg = dict(sizes=sizes, nb=nb, kern_width=kern_width, step_size=step_size)
    n1, n2 = n_chip, n_chip
    vmem = pl.BlockSpec(memory_space=pltpu.VMEM)
    most1 = max(n_chip // sizes[k] for k in range(3))
    most2 = max(sizes)
    scratch = [
        pltpu.VMEM((n_total, fcol), BF16),
        pltpu.VMEM((n_total, fcol), BF16),
        pltpu.VMEM((n_total, fcol), BF16),
        pltpu.VMEM((rank, n_total), F32),
        pltpu.VMEM((rank // 2, n_total), F32),
        pltpu.VMEM((rank, n_total), F32),
        pltpu.VMEM((nb, 8, B), F32),
        pltpu.VMEM((3, n_chip, PIECE, B), F32),
        pltpu.VMEM((3, 4, most1, PIECE, B), F32),
        pltpu.VMEM((3, 4, most2, PIECE, B), F32),
        pltpu.VMEM((3, 4, PIECE, B), F32),
        pltpu.VMEM((3, most1, PIECE, B), F32),
        pltpu.VMEM((3, most2, PIECE, B), F32),
        pltpu.VMEM((3, PIECE, B), F32),
        pltpu.VMEM((3, n_chip, PIECE, B), BF16),
        pltpu.VMEM((3, n_chip, PIECE, B), BF16),
        pltpu.VMEM((n_total, n_total), BF16),
        pltpu.SemaphoreType.DMA((NUM_SEMS,)),
        pltpu.SemaphoreType.DMA((NUM_SEMS,)),
    ]
    return pl.pallas_call(
        functools.partial(steps_kernel, cfg),
        out_shape=jax.ShapeDtypeStruct(theta.shape, F32),
        in_specs=[vmem] * 5,
        out_specs=vmem,
        scratch_shapes=scratch,
        compiler_params=pltpu.CompilerParams(collective_id=0, has_side_effects=True, vmem_limit_bytes=60 * 1024 * 1024),
        name="svgd_steps",
    )(theta, lam[None], mu[None], fac, fac.T)


def solution(mesh, sizes=(4, 4, 4)):
    part_size = mesh.shape["part"]
    feat_size = mesh.shape["feat"]

    def local_steps(local_theta, prec_loc, mean_loc, factor_loc):
        rows_loc, feat_loc = local_theta.shape
        n_total = rows_loc * part_size
        feat_total = feat_loc * feat_size
        kern_width = 2.0 * feat_total / math.log(n_total)
        step_size = 0.15 * n_total * feat_total / math.log(n_total)
        part_idx = lax.axis_index("part")
        fcol = feat_loc // part_size
        theta = lax.all_to_all(local_theta, "part", split_axis=1, concat_axis=0, tiled=True)
        lam = lax.dynamic_slice_in_dim(prec_loc, part_idx * fcol, fcol)
        mu = lax.dynamic_slice_in_dim(mean_loc, part_idx * fcol, fcol)
        fac = lax.dynamic_slice_in_dim(factor_loc, part_idx * fcol, fcol)
        theta = run_steps(theta, lam, mu, fac, sizes, kern_width, step_size)
        return lax.all_to_all(theta, "part", split_axis=0, concat_axis=1, tiled=True)

    row_spec = P(("ens", "part"), "feat")
    vec_spec = P(("ens", "feat"))
    fac_spec = P(("ens", "feat"), None)
    return jax.shard_map(local_steps, mesh=mesh, in_specs=(row_spec, vec_spec, vec_spec, fac_spec), out_specs=row_spec, check_vma=False)
```

time: 969 us -> 362 us (0.37)
  waiting for transfers between devices: 744 us -> 27 us
  Pallas kernels: 0 us -> 289 us
  matrix products: 101 us -> 0 us
  blocking collectives: 78.6 us -> 27.4 us
  other arithmetic: 29.7 us -> 0 us
  between operations: 13.4 us -> 0.03 us
  local copies, waits for them, and re-layouts: 0.28 us -> 10.1 us
    all_gather x6 -> x0, waiting for transfers between devices: 662 us -> none  [the longest x3 332 us: local_steps(): grad_all = lax.all_gather(grad_b, 'part', axis=0, tiled=True)]
    pallas_call x0 -> x1, Pallas kernels: none -> 289 us  [run_steps(): pl.pallas_call(functools.partial(steps_kernel, cfg), out_shape=jax.ShapeD...]
    dot_general x15 -> x0, matrix products: 101 us -> none  [the longest x3 37.1 us: local_steps(): jnp.einsum('nd,md->nm', theta_b, theta_all, preferred_element_type=jnp.fl...]
    psum x3 -> x0, waiting for transfers between devices: 81.6 us -> none  [local_steps(): gram_rows, sq_norm = lax.psum((gram_part, sq_part), 'feat')]
    psum x3 -> x0, blocking collectives: 78.6 us -> none  [local_steps(): gram_rows, sq_norm = lax.psum((gram_part, sq_part), 'feat')]
    all_to_all x0 -> x1, blocking collectives: none -> 27.4 us  [local_steps(): lax.all_to_all(theta, 'part', split_axis=0, concat_axis=1, tiled=True)]
    all_to_all x0 -> x1, waiting for transfers between devices: none -> 27 us  [local_steps(): lax.all_to_all(local_theta, 'part', split_axis=1, concat_axis=0, tiled=True)]
    dot_general x3 -> x0, other arithmetic: 21.9 us -> none  [local_steps(): jnp.einsum('md,md->m', theta_all, theta_all, preferred_element_type=jnp.f...]
  transfers between devices with their start and end apart: 9 -> 1, of which waited for: 9 -> 1; matrix products, arithmetic and copies ran while one was open for 4% -> 1% of each run, Pallas kernels for 0% -> 0%
where the time goes in v1:
time: 362 us; the launch traced here: 361 us
  Pallas kernels  289 us (80%)
  blocking collectives  27.4 us (8%)
  waiting for transfers between devices  27 us (7%)
  local copies, waits for them, and re-layouts  10.1 us (3%)
  starting transfers between devices  8.19 us (2%)
    pallas_call x1, Pallas kernels, run_steps(): pl.pallas_call(functools.partial(steps_kernel, cfg), out_shape=jax.ShapeD...  289 us
    all_to_all x1, blocking collectives, local_steps(): lax.all_to_all(theta, 'part', split_axis=0, concat_axis=1, tiled=True)  27.4 us
    all_to_all x1, waiting for transfers between devices, local_steps(): lax.all_to_all(local_theta, 'part', split_axis=1, concat_axis=0, tiled=True)  27 us
    all_to_all x1, starting transfers between devices, local_steps(): lax.all_to_all(local_theta, 'part', split_axis=1, concat_axis=0, tiled=True)  8.19 us
  transfers between devices with their start and end apart: 1, of which 1 were waited for; matrix products, arithmetic and copies ran while one was open for 1% of the time, Pallas kernels for 0%

profile of v1, /device:TPU:0, one launch (start us, length us, event | category | flops | bytes accessed | tf_op | source)
XLA Modules:
  0.0 361.4 jit_solution(3192616644140177560)
XLA Ops:
  0.0 0.0 copy-start
  0.0 3.2 copy.11
  3.2 8.2 %all-to-all-start = ((f32[128,16,256]{2,0,1:T(8,128)}), f32[128,16,256]{2,0,1:T(8,128)S(1)}, u32[]{:S(2)}, u32[]{:S(2)}) async-start(f32[128,16,256]{2,0,1:T(8,128)} %bitcast.16), calls=%async_computation | async-start | bytes 4194304 | tf_op jit(solution)/shard_map/all_to_all | solution.py:389
  11.4 1.3 dynamic_slice.9
  12.7 1.3 dynamic_slice.10
  14.1 0.0 copy-done
  14.1 0.7 copy.6.fac_ref
  14.8 0.6 fusion.fact_ref
  15.4 27.0 %all-to-all-done = f32[128,16,256]{2,0,1:T(8,128)S(1)} async-done(((f32[128,16,256]{2,0,1:T(8,128)}), f32[128,16,256]{2,0,1:T(8,128)S(1)}, u32[]{:S(2)}, u32[]{:S(2)}) %all-to-all-start) | async-done | bytes 2097184 | tf_op jit(solution)/shard_map/all_to_all | solution.py:389
  42.5 0.0 copy-start.1
  42.5 1.3 copy-done.1
  43.8 288.6 %svgd_steps.1 = f32[2048,256]{1,0:T(8,128)} custom-call(f32[2048,256]{1,0:T(8,128)} %bitcast.15, f32[1,256]{1,0:T(1,128)} %bitcast.20, f32[1,256]{1,0:T(1,128)} %bitcast.21, bf16[256,64]{1,0:T(8,128)(2,1)} %copy.6.fac_ref, bf16[64,256]{1,0:T(8,128)(2,1)} %fusion.fact_ref), custom_call_target="tpu_custom_call" | custom-call | tf_op jit(solution)/shard_map/svgd_steps/pallas_call | solution.py:366
  332.4 27.4 %all_to_all.38 = f32[16,128,256]{2,1,0:T(8,128)S(1)} all-to-all(f32[16,128,256]{2,1,0:T(8,128)} %bitcast.17), channel_id=1, replica_groups=mesh['ens'=1,'part'=16,'feat'=8] {'part'}, dimensions={0} | all-to-all | bytes 4194304 | tf_op jit(solution)/shard_map/all_to_all | solution.py:394
  359.9 1.5 copy.9
  (1 shorter events, 0.0 us)
Async XLA Ops:
  0.0 14.1 %copy-start = (bf16[4096,64]{0,1:T(8,128)(2,1)S(1)}, bf16[4096,64]{0,1:T(8,128)(2,1)}, u32[]{:S(2)}) copy-start(bf16[4096,64]{0,1:T(8,128)(2,1)} %param.7) | copy-start | bytes 1572868
  3.2 39.3 %all-to-all-start = ((f32[128,16,256]{2,0,1:T(8,128)}), f32[128,16,256]{2,0,1:T(8,128)S(1)}, u32[]{:S(2)}, u32[]{:S(2)}) async-start(f32[128,16,256]{2,0,1:T(8,128)} %bitcast.16), calls=%async_computation | async-start | bytes 4194304 | tf_op jit(solution)/shard_map/all_to_all | solution.py:389
  42.5 1.3 copy-start.1
